TPU v7x, 256 devices: a whole 4x4x8 slice. The times are simulated.
256 devices in a mesh: bank: 16 (over z, core), zero: 16 (over y, x).
Axes of the slice: x: 4, y: 4, z: 8, core: 2. Of those that a mesh axis runs over, the one named last changes fastest.
Arguments:
- master_down: float32 [64, 1024, 2048], P('bank', None, 'zero'), may hold values from -0.25 to 0.25
- second_down: bfloat16 [64, 1024, 2048], P('bank', None, 'zero'), may hold values from -0.09375 to 0.09375
- router_weight: float32 [2048, 64], P('zero', 'bank'), may hold values from -0.125 to 0.125
- router_gain: float32 [2048], P('zero'), may hold values from 0.25 to 1.75
Outputs:
- final_down: bfloat16 [64, 1024, 2048], P('bank')
- scale_down: float32 [64, 1024], P('bank')
- serve_router: bfloat16 [2048, 64], replicated
All inputs are finite; a program needn't handle non-finite values. Where the computation divides by a largest or mean magnitude, that divisor is 1e-20 or more.
Results may differ from a plain program's by a relative error of at most 0.001.
Values may be sent and summed in bfloat16 or wider, within the bound.
A program may use at most 128 MiB of HBM per device.

v0:
```python
import jax
import jax.numpy as jnp
from jax import lax
from jax.sharding import PartitionSpec as P


def from_everyone(value, axis):
    count = lax.axis_size(axis)
    return lax.all_to_all(
        jnp.broadcast_to(value[None], (count, *value.shape)), axis, 0, 0, tiled=True
    )


def over_copies(value, axis):
    everything = from_everyone(value, axis)
    return jnp.max(everything, axis=0)


def joined_along(pieces, dim):
    pieces = jnp.moveaxis(pieces, 0, dim)
    dims = pieces.shape
    return pieces.reshape(*dims[:dim], dims[dim] * dims[dim + 1], *dims[dim + 2 :])


def collect(value, axis, dim):
    return joined_along(from_everyone(value, axis), dim)


def shards(master_down, second_down, router_weight, router_gain):
    merged_down = master_down + second_down.astype(jnp.float32)
    scale_down = over_copies(jnp.max(jnp.abs(merged_down), axis=2), "zero")
    narrow_down = (merged_down / jnp.expand_dims(scale_down, 2)).astype(jnp.bfloat16)
    final_down = lax.all_gather(narrow_down, "zero", axis=2, tiled=True)
    part_router = (router_weight * router_gain[:, None]).astype(jnp.bfloat16)
    row_router = collect(part_router, "zero", 0)
    serve_router = lax.all_gather(row_router, "bank", axis=1, tiled=True)
    return (final_down, scale_down, serve_router)


def solution(mesh):
    return jax.shard_map(
        shards,
        mesh=mesh,
        in_specs=(P("bank", None, "zero"), P("bank", None, "zero"), P("zero", "bank"), P("zero")),
        out_specs=(P("bank", None, None), P("bank", None), P()),
        check_vma=False,
    )
```

profile of v0, /device:TPU:2, one launch (start us, length us, event | category | flops | bytes accessed | tf_op | source)
XLA Modules:
  0.0 171.8 jit_solution(3253551120182133146)
XLA Ops:
  7.2 0.0 copy-start
  7.2 0.0 copy-start.1
  7.2 0.0 all-gather.3.cloned.1.call-start
  7.2 2.6 %abs_reduce_fusion = f32[4,1024]{1,0:T(4,128)S(1)} fusion(f32[4,1024,128]{2,1,0:T(8,128)} %param.4, bf16[4,1024,128]{2,1,0:T(8,128)(2,1)} %param.5), kind=kLoop, calls=%fused_computation.1 | loop fusion | flops 2093056 | bytes 3162112 | tf_op jit(solution)/shard_map/reduce_max | solution.py:31
  9.9 14.6 %all_to_all.10 = f32[16,4,1024]{2,1,0:T(4,128)S(1)} all-to-all(f32[16,4,1024]{2,1,0:T(4,128)S(1)} %broadcast_in_dim.4), channel_id=1, replica_groups=mesh['bank'=16,'zero'=16] {'zero'}, dimensions={0} | all-to-all | bytes 524288 | tf_op jit(solution)/shard_map/all_to_all | solution.py:9
  24.5 0.1 reduce_max.19
  24.6 0.0 copy-done
  24.6 0.0 copy-done.1
  24.6 0.0 copy-start.2
  24.6 0.0 copy-start.3
  24.6 0.0 copy-start.4
  24.6 1.5 divide_convert_fusion
  26.1 0.0 copy-done.2
  26.1 0.0 all-gather.3.cloned.1.call-update
  26.2 0.0 copy-done.3
  26.2 0.0 copy-done.4
  26.2 10.5 %all_to_all.11 = bf16[16,128,4]{1,2,0:T(4,128)(2,1)S(1)} all-to-all(bf16[16,128,4]{1,2,0:T(4,128)(2,1)S(1)} %broadcast_in_dim.5), channel_id=1, replica_groups=mesh['bank'=16,'zero'=16] {'zero'}, dimensions={0} | all-to-all | bytes 32768 | tf_op jit(solution)/shard_map/all_to_all | solution.py:9
  36.7 20.7 %all-gather = bf16[16,4,2048]{2,1,0:T(4,128)(2,1)S(1)} all-gather(bf16[1,4,2048]{2,1,0:T(4,128)(2,1)S(1)} %bitcast.7), channel_id=1, replica_groups=mesh['bank'=16,'zero'=16] {'bank'}, dimensions={0}, use_global_device_ids=true | all-gather | bytes 278528 | tf_op jit(solution)/shard_map/all_gather | solution.py:36
  57.4 0.8 reshape.15
  58.1 92.7 %all-gather.3.cloned.1.call-done = bf16[4,1024,2048]{2,1,0:T(8,128)(2,1)} async-done(((bf16[4,1024,128]{2,1,0:T(8,128)(2,1)}), bf16[4,1024,2048]{2,1,0:T(8,128)(2,1)}) %all-gather.3.cloned.1.call-update) | async-done | bytes 16777232 | tf_op jit(solution)/shard_map/all_gather | solution.py:33
  150.8 14.2 %copy.10 = bf16[4,1024,2048]{2,1,0:T(8,128)(2,1)} copy(bf16[4,1024,2048]{2,1,0:T(8,128)(2,1)} %all-gather.3.cloned.1.call-done) | data formatting | bytes 33554432
  (3 shorter events, 0.1 us)
Async XLA Ops:
  7.2 17.4 %copy-start = (f32[4,1024,128]{2,1,0:T(8,128)S(1)}, f32[4,1024,128]{2,1,0:T(8,128)}, u32[]{:S(2)}) copy-start(f32[4,1024,128]{2,1,0:T(8,128)} %param.4) | copy-start | bytes 6291460
  7.2 17.4 %copy-start.1 = (bf16[4,1024,128]{2,1,0:T(8,128)(2,1)S(1)}, bf16[4,1024,128]{2,1,0:T(8,128)(2,1)}, u32[]{:S(2)}) copy-start(bf16[4,1024,128]{2,1,0:T(8,128)(2,1)} %param.5) | copy-start | bytes 3145732
  7.2 143.6 %all-gather.3.cloned.1.call-start = ((), (), s32[]{:S(2)}) async-start(), calls=%async_computation.2 | async-start | bytes 17825792 | tf_op jit(solution)/shard_map/all_gather | solution.py:33
  24.6 1.6 copy-start.2
  24.6 1.6 copy-start.3
  24.6 1.6 copy-start.4
Sparse Core Ops, SparseCore 0:
  26.3 124.4 all-gather.2
where the time goes:
time: 172 us
  waiting for transfers between devices  92.7 us (54%)
  blocking collectives  45.8 us (27%)
  local copies, waits for them, and re-layouts  15 us (9%)
  between operations  14.1 us (8%)
  other arithmetic  4.21 us (2%)
    all_gather x1, waiting for transfers between devices, shards(): final_down = lax.all_gather(narrow_down, 'zero', axis=2, tiled=True)  92.7 us
    all_to_all x2, blocking collectives, from_everyone(): lax.all_to_all(jnp.broadcast_to(value[None], (count, *value.shape)), axis...  25.1 us
    all_gather x1, blocking collectives, shards(): serve_router = lax.all_gather(row_router, 'bank', axis=1, tiled=True)  20.7 us
    unnamed x12, local copies, waits for them, and re-layouts  14.9 us
  transfers between devices with their start and end apart: 1, of which 1 were waited for; matrix products, arithmetic and copies ran while one was open for 0% of the time, Pallas kernels for 0%

commit v1 on v0

v1 whole, which is shorter than its diff:
```python
import jax
import jax.numpy as jnp
from jax import lax
from jax.experimental import pallas as pl
from jax.experimental.pallas import tpu as pltpu
from jax.sharding import PartitionSpec as P

SIDE = 4
PLANE = SIDE * SIDE
PIECES = 8
LEAD = 3
MESH = pl.DeviceIdType.MESH
F32 = jnp.float32
BF16 = jnp.bfloat16


def routes(piece, origin, via):
    turned, half = piece % 2, (piece // 2) % 2
    first, second = origin if not turned else origin[::-1]
    if via is None:
        legs = [(0, 3), (1, 3), (2, 1 - half), (3, half)]
    else:
        along = via ^ (2 * turned)
        if along < 2:
            legs = [(2, 1 - half), (3, half)]
            if (along, first, half) in ((0, SIDE - 1, 0), (1, 1, 1)):
                legs.append((along, 2))
        elif (along, second, half) in ((2, SIDE - 1, 0), (3, 1, 1)):
            legs = [(along, 0)]
        else:
            legs = []
    return [(direction ^ (2 * turned), weight) for direction, weight in legs]


STEP = ((-1, 0), (1, 0), (0, -1), (0, 1))


def schedule():
    waiting = [[] for _ in range(4)]
    order = [[] for _ in range(4)]
    for piece in range(PIECES):
        for direction, weight in routes(piece, (0, 0), None):
            waiting[direction].append((-weight, 0, piece, (0, 0)))

    def pick():
        for direction in range(4):
            if waiting[direction]:
                best = min(waiting[direction])
                waiting[direction].remove(best)
                order[direction].append(best[2:])

    for _ in range(LEAD):
        pick()
    for turn in range((PLANE - 1) * PIECES // 4):
        for direction in range(4):
            piece, origin = order[direction][turn]
            origin = tuple((o + s) % SIDE for o, s in zip(origin, STEP[direction]))
            for onward, weight in routes(piece, origin, direction):
                waiting[onward].append((-weight, turn + 1, piece, origin))
        pick()
    return order


ORDER = schedule()
TURNS = (PLANE - 1) * PIECES // 4
assert all(len(lane) == TURNS for lane in ORDER)


def exchange(
    master, second, weight, gain, slab, scale_out, router_out,
    merged, change, weight_in, gain_in, tops, inverse, columns, banks, wide,
    load_sem, tops_send, tops_recv, send_sem, recv_sem, ring_send, ring_recv, pair_send, pair_recv,
):
    experts, rows, lanes = master.shape
    per_piece = experts * rows // PIECES
    bank_count = banks.shape[0]
    me = lax.axis_index("zero")
    bank = lax.axis_index("bank")
    my_x, my_y = lax.rem(me, SIDE), lax.div(me, SIDE)

    def at(x, y):
        return lax.rem(my_y + y, SIDE) * SIDE + lax.rem(my_x + x, SIDE)

    neighbour = (at(1, 0), at(SIDE - 1, 0), at(0, 1), at(0, SIDE - 1))
    above = lax.rem(bank + 2, bank_count)
    below = lax.rem(bank + bank_count - 2, bank_count)
    partner = bank + 1 - 2 * lax.rem(bank, 2)

    loads = []
    for e in range(experts):
        loads.append(
            (
                pltpu.make_async_copy(master.at[e], merged.at[e], load_sem.at[2 * e]),
                pltpu.make_async_copy(second.at[e], change.at[e], load_sem.at[2 * e + 1]),
            )
        )
        for load in loads[-1]:
            load.start()
    small = (
        pltpu.make_async_copy(weight, weight_in, load_sem.at[2 * experts]),
        pltpu.make_async_copy(gain, gain_in, load_sem.at[2 * experts + 1]),
    )
    for load in small:
        load.start()

    barrier = pltpu.get_barrier_semaphore()
    others = [at(x, y) for y in range(SIDE) for x in range(SIDE) if (x, y) != (0, 0)]
    for other in others:
        pl.semaphore_signal(barrier, inc=1, device_id={"zero": other}, device_id_type=MESH)
    for other in (above, below, partner):
        pl.semaphore_signal(barrier, inc=1, device_id={"bank": other}, device_id_type=MESH)

    lane = lax.broadcasted_iota(jnp.int32, (8, lanes), 1)
    groups = rows // 16

    def find_tops(e):
        for load in loads[e]:
            load.wait()

        def body(g, top):
            at_rows = pl.ds(pl.multiple_of(g * 16, 16), 16)
            total = merged[e, at_rows, :] + change[e, at_rows, :].astype(F32)
            merged[e, at_rows, :] = total
            peak = jnp.max(jnp.abs(total), axis=1, keepdims=True)
            top = jnp.where(lane == 2 * g, peak[:8], top)
            return jnp.where(lane == 2 * g + 1, peak[8:], top)

        tops[me, e] = lax.fori_loop(0, groups, body, jnp.zeros((8, lanes), F32), unroll=8)

    def share_tops(first, last, message):
        sends = []
        for i, other in enumerate(others):
            part = tops.at[me, pl.ds(first, last - first)]
            sends.append(
                pltpu.make_async_remote_copy(
                    part, part, tops_send.at[message, i], tops_recv.at[message, i],
                    device_id={"zero": other}, device_id_type=MESH,
                )
            )
            sends[-1].start()
        return sends

    def divide(e):
        top = jnp.max(tops[:, e], axis=0)
        columns[e] = top
        inverse[...] = 1.0 / top

        def body(g, carry):
            here = pltpu.roll(inverse[...], lax.rem(lanes - 8 * g, lanes), 1)
            for i in range(4):
                at_rows = pl.ds(pl.multiple_of(g * 64 + 16 * i, 16), 16)
                low = jnp.broadcast_to(here[:, 2 * i : 2 * i + 1], (8, lanes))
                high = jnp.broadcast_to(here[:, 2 * i + 1 : 2 * i + 2], (8, lanes))
                value = merged[e, at_rows, :] * jnp.concatenate([low, high], axis=0)
                to_rows = pl.ds(pl.multiple_of(e * rows + g * 64 + 16 * i, 16), 16)
                slab[me, to_rows, :] = value.astype(BF16)
            return carry

        lax.fori_loop(0, groups // 4, body, 0, unroll=2)

    find_tops(0)
    pl.semaphore_wait(barrier, PLANE - 1 + 3)
    top_sends = share_tops(0, 1, 0)
    for e in range(1, experts):
        find_tops(e)
    for load in small:
        load.wait()
    tops[me, experts, 0:4, :] = weight_in[...] * gain_in[...]
    tops[me, experts, 4:8, :] = jnp.zeros((4, lanes), F32)
    late_sends = share_tops(1, experts + 1, 1)

    in_flight = []

    def send(direction, turn):
        piece, (x, y) = ORDER[direction][turn]
        part = slab.at[at(x, y), pl.ds(piece * per_piece, per_piece)]
        copy = pltpu.make_async_remote_copy(
            part, part, send_sem.at[direction, turn], recv_sem.at[direction, turn],
            device_id={"zero": neighbour[direction]}, device_id_type=MESH,
        )
        copy.start()
        in_flight.append(copy)

    def receive(direction, turn):
        piece, origin = ORDER[direction][turn]
        x, y = (o + s for o, s in zip(origin, STEP[direction]))
        part = slab.at[at(x + SIDE, y + SIDE), pl.ds(piece * per_piece, per_piece)]
        pltpu.make_async_remote_copy(
            part, part, send_sem.at[direction, turn], recv_sem.at[direction, turn],
            device_id={"zero": neighbour[direction]}, device_id_type=MESH,
        ).wait_recv()

    done = 0

    def ready(upto):
        nonlocal done
        while done < min(upto, experts):
            if done < 2:
                for copy in (top_sends, late_sends)[done]:
                    copy.wait_recv()
            divide(done)
            done += 1

    for turn in range(LEAD):
        needed = max(ORDER[d][turn][0] for d in range(4) if ORDER[d][turn][1] == (0, 0))
        ready(needed * per_piece // rows + 1)
        for direction in range(4):
            send(direction, turn)
    ready(experts)

    ring_copies, pair_copies = [], []

    def own_bank():
        for j in range(PLANE):
            banks[bank, :, lanes * j : lanes * (j + 1)] = tops[j, experts, 0:4, :]

    def bank_at(shift):
        return lax.rem(bank + bank_count + shift, bank_count)

    def ring(step):
        for way, shift, other in ((0, -2, above), (1, 2, below)):
            if step > (4 if way == 0 else 3):
                continue
            part = banks.at[bank_at(shift * (step - 1))]
            copy = pltpu.make_async_remote_copy(
                part, part, ring_send.at[way, step - 1], ring_recv.at[way, step - 1],
                device_id={"bank": other}, device_id_type=MESH,
            )
            copy.start()
            ring_copies.append(copy)

    def ring_arrived(step):
        for copy in ring_copies[2 * (step - 1) : 2 * step]:
            copy.wait_recv()

    def pair(step):
        shifts = (0,) if step == 0 else (-2 * step, 2 * step) if step < 4 else (-2 * step,)
        for shift in shifts:
            part = banks.at[bank_at(shift)]
            n = len(pair_copies)
            copy = pltpu.make_async_remote_copy(
                part, part, pair_send.at[n], pair_recv.at[n],
                device_id={"bank": partner}, device_id_type=MESH,
            )
            copy.start()
            pair_copies.append(copy)

    def finish_scale():
        for e in range(experts):
            wide[0:lanes, 0:8] = jnp.transpose(columns[e])
            line = jnp.zeros((8, lanes), F32)
            for q in range(16):
                part = wide[pl.ds(q, 8, stride=16), 0:lanes]
                part = pltpu.roll(part, 8 * q, 1) if q else part
                line = jnp.where((lane >= 8 * q) & (lane < 8 * q + 8), part, line)
            for r in range(8):
                scale_out[e : e + 1, lanes * r : lanes * (r + 1)] = line[r : r + 1, :]

    def finish_router():
        for copy in pair_copies:
            copy.wait_recv()
        for b in range(bank_count):
            router_out[4 * b : 4 * b + 4, :] = banks[b]

    def ring_step(step):
        def run():
            ring_arrived(step)
            if step < 4:
                ring(step + 1)
            pair(step)

        return run

    def first_step():
        own_bank()
        ring(1)
        pair(0)

    every = TURNS // 10
    extras = {
        1: finish_scale,
        every: first_step,
        2 * every: ring_step(1),
        3 * every: ring_step(2),
        4 * every: ring_step(3),
        5 * every: ring_step(4),
        6 * every: finish_router,
    }

    for turn in range(TURNS):
        for direction in range(4):
            receive(direction, turn)
        if turn + LEAD < TURNS:
            for direction in range(4):
                send(direction, turn + LEAD)
        if turn in extras:
            extras[turn]()
    for copy in in_flight + top_sends + late_sends + ring_copies + pair_copies:
        copy.wait_send()


def store(slab, scale_in, router_in, final, scale, router, half, sem):
    experts, rows, width = final.shape
    lanes = width // PLANE
    copies = []
    for e in range(experts):
        for j in range(PLANE):
            copies.append(
                pltpu.make_async_copy(
                    slab.at[j, pl.ds(e * rows, rows)],
                    final.at[e, :, pl.ds(j * lanes, lanes)],
                    sem.at[e * PLANE + j],
                )
            )
    for copy in copies:
        copy.start()
    half[...] = router_in[...].astype(BF16)
    copies.append(pltpu.make_async_copy(scale_in, scale, sem.at[experts * PLANE]))
    copies.append(pltpu.make_async_copy(half, router, sem.at[experts * PLANE + 1]))
    copies[-2].start()
    copies[-1].start()
    for copy in copies:
        copy.wait()


def shards(master, second, weight, gain):
    experts, rows, lanes = master.shape
    banks = lax.axis_size("bank")
    width = lanes * PLANE
    hbm = pl.BlockSpec(memory_space=pltpu.HBM)
    vmem = pl.BlockSpec(memory_space=pltpu.VMEM)
    dma = pltpu.SemaphoreType.DMA
    values = (master, second, weight.T, gain.reshape(1, lanes))
    slab, scale, router = pl.pallas_call(
        exchange,
        out_shape=(
            pltpu.VMEM((PLANE, experts * rows, lanes), BF16),
            pltpu.VMEM((experts, rows), F32),
            pltpu.VMEM((banks * experts, width), F32),
        ),
        in_specs=[hbm] * 4,
        out_specs=(vmem,) * 3,
        scratch_shapes=[
            pltpu.VMEM((experts, rows, lanes), F32),
            pltpu.VMEM((experts, rows, lanes), BF16),
            pltpu.VMEM((experts, lanes), F32),
            pltpu.VMEM((1, lanes), F32),
            pltpu.VMEM((PLANE, experts + 1, 8, lanes), F32),
            pltpu.VMEM((8, lanes), F32),
            pltpu.VMEM((experts, 8, lanes), F32),
            pltpu.VMEM((banks, experts, width), F32),
            pltpu.VMEM((lanes, lanes), F32),
            dma((2 * experts + 2,)),
            dma((2, PLANE - 1)),
            dma((2, PLANE - 1)),
            dma((4, TURNS)),
            dma((4, TURNS)),
            dma((2, 4)),
            dma((2, 4)),
            dma((8,)),
            dma((8,)),
        ],
        compiler_params=pltpu.CompilerParams(
            collective_id=0, has_side_effects=True, vmem_limit_bytes=24 << 20
        ),
        name="exchange",
    )(*(pltpu.with_memory_space_constraint(value, pltpu.HBM) for value in values))
    final, scale, router = pl.pallas_call(
        store,
        out_shape=(
            jax.ShapeDtypeStruct((experts, rows, width), BF16),
            jax.ShapeDtypeStruct((experts, rows), F32),
            jax.ShapeDtypeStruct((banks * experts, width), BF16),
        ),
        in_specs=[vmem] * 3,
        out_specs=(hbm,) * 3,
        scratch_shapes=[
            pltpu.VMEM((banks * experts, width), BF16),
            dma((experts * PLANE + 2,)),
        ],
        compiler_params=pltpu.CompilerParams(vmem_limit_bytes=4 << 20),
        name="store",
    )(slab, scale, router)
    return final, scale, router.T


def solution(mesh):
    return jax.shard_map(
        shards,
        mesh=mesh,
        in_specs=(P("bank", None, "zero"), P("bank", None, "zero"), P("zero", "bank"), P("zero")),
        out_specs=(P("bank", None, None), P("bank", None), P()),
        check_vma=False,
    )
```

time: 172 us -> 111 us (0.65)
  Pallas kernels: 0 us -> 110 us
  waiting for transfers between devices: 92.7 us -> 0 us
  blocking collectives: 45.8 us -> 0 us
  local copies, waits for them, and re-layouts: 15 us -> 0 us
  between operations: 14.1 us -> 0.64 us
  other arithmetic: 4.21 us -> 0 us
    pallas_call x0 -> x2, Pallas kernels: none -> 110 us  [the longest x1 103 us: shards(): pl.pallas_call(exchange, out_shape=(pltpu.VMEM((PLANE, experts * rows, la...]
    all_gather x1 -> x0, waiting for transfers between devices: 92.7 us -> none  [shards(): final_down = lax.all_gather(narrow_down, 'zero', axis=2, tiled=True)]
    all_to_all x2 -> x0, blocking collectives: 25.1 us -> none  [from_everyone(): lax.all_to_all(jnp.broadcast_to(value[None], (count, *value.shape)), axis...]
    all_gather x1 -> x0, blocking collectives: 20.7 us -> none  [shards(): serve_router = lax.all_gather(row_router, 'bank', axis=1, tiled=True)]
    unnamed x12 -> x0, local copies, waits for them, and re-layouts: 14.9 us -> none
    reduce_max x2 -> x0, other arithmetic: 2.68 us -> none  [the longest x1 2.63 us: shards(): scale_down = over_copies(jnp.max(jnp.abs(merged_down), axis=2), 'zero')]
  transfers between devices with their start and end apart: 1 -> 0, of which waited for: 1 -> 0; matrix products, arithmetic and copies ran while one was open for 0% -> 0% of each run, Pallas kernels for 0% -> 0%
where the time goes in v1:
time: 111 us; the launch traced here: 110 us
  Pallas kernels  110 us (99%)
    pallas_call x1, Pallas kernels, shards(): pl.pallas_call(exchange, out_shape=(pltpu.VMEM((PLANE, experts * rows, la...  103 us
    pallas_call x1, Pallas kernels, shards(): pl.pallas_call(store, out_shape=(jax.ShapeDtypeStruct((experts, rows, wid...  6.44 us

profile of v1, /device:TPU:2, one launch (start us, length us, event | category | flops | bytes accessed | tf_op | source)
XLA Modules:
  0.0 110.4 jit_solution(5802214296427907506)
XLA Ops:
  0.6 103.4 %exchange.1 = (bf16[16,4096,128]{2,1,0:T(8,128)(2,1)S(1)}, f32[4,1024]{1,0:T(4,128)S(1)}, f32[64,2048]{1,0:T(8,128)S(1)}) custom-call(f32[4,1024,128]{2,1,0:T(8,128)} %master.1, bf16[4,1024,128]{2,1,0:T(8,128)(2,1)} %second.1, f32[4,128]{1,0:T(4,128)} %bitcast.3, f32[1,128]{1,0:T(1,128)} %bitcast.4), custom_call_target="tpu_custom_call" | custom-call | tf_op jit(solution)/shard_map/exchange/pallas_call | solution.py:334
  104.0 6.4 %store.1 = (bf16[4,1024,2048]{2,1,0:T(8,128)(2,1)}, f32[4,1024]{1,0:T(4,128)}, bf16[64,2048]{1,0:T(8,128)(2,1)}) custom-call(bf16[16,4096,128]{2,1,0:T(8,128)(2,1)S(1)} %get-tuple-element.9.slab, f32[4,1024]{1,0:T(4,128)S(1)} %get-tuple-element.10.scale_in, f32[64,2048]{1,0:T(8,128)S(1)} %get-tuple-element.11.router_in), custom_call_target="tpu_custom_call" | custom-call | tf_op jit(solution)/shard_map/store/pallas_call | solution.py:368

commit v2 on v1

--- a/solution.py
+++ b/solution.py
@@ -7,8 +7,9 @@
 
 SIDE = 4
 PLANE = SIDE * SIDE
+EXPERTS = 4
 PIECES = 8
-LEAD = 3
+LEAD = 4
 MESH = pl.DeviceIdType.MESH
 F32 = jnp.float32
 BF16 = jnp.bfloat16
@@ -44,8 +45,10 @@
 
     def pick():
         for direction in range(4):
-            if waiting[direction]:
-                best = min(waiting[direction])
+            limit = (len(order[direction]) // 2 + 1) * PIECES // EXPERTS
+            now = [entry for entry in waiting[direction] if entry[2] < limit or entry[1]]
+            if now:
+                best = min(now)
                 waiting[direction].remove(best)
                 order[direction].append(best[2:])
 
@@ -68,8 +71,8 @@
 
 def exchange(
     master, second, weight, gain, slab, scale_out, router_out,
-    merged, change, weight_in, gain_in, tops, inverse, columns, banks, wide,
-    load_sem, tops_send, tops_recv, send_sem, recv_sem, ring_send, ring_recv, pair_send, pair_recv,
+    merged, change, weight_in, gain_in, tops, part_router, inverse, columns, banks, wide,
+    load_sem, tops_send, tops_recv, hello, send_sem, recv_sem, ring_send, ring_recv, pair_send, pair_recv,
 ):
     experts, rows, lanes = master.shape
     per_piece = experts * rows // PIECES
@@ -107,8 +110,20 @@
     others = [at(x, y) for y in range(SIDE) for x in range(SIDE) if (x, y) != (0, 0)]
     for other in others:
         pl.semaphore_signal(barrier, inc=1, device_id={"zero": other}, device_id_type=MESH)
-    for other in (above, below, partner):
-        pl.semaphore_signal(barrier, inc=1, device_id={"bank": other}, device_id_type=MESH)
+    floor, core = lax.div(bank, 2), lax.rem(bank, 2)
+    last = bank_count // 2 - 1
+
+    def greet(semaphore, condition, other):
+        @pl.when(condition)
+        def _():
+            pl.semaphore_signal(semaphore, inc=1, device_id={"bank": other}, device_id_type=MESH)
+
+    def flag(condition):
+        return jnp.where(condition, 1, 0)
+
+    greet(barrier, floor < last, above)
+    greet(barrier, floor == 0, below)
+    greet(barrier, core == 0, partner)
 
     lane = lax.broadcasted_iota(jnp.int32, (8, lanes), 1)
     groups = rows // 16
@@ -125,23 +140,22 @@
             top = jnp.where(lane == 2 * g, peak[:8], top)
             return jnp.where(lane == 2 * g + 1, peak[8:], top)
 
-        tops[me, e] = lax.fori_loop(0, groups, body, jnp.zeros((8, lanes), F32), unroll=8)
-
-    def share_tops(first, last, message):
-        sends = []
-        for i, other in enumerate(others):
-            part = tops.at[me, pl.ds(first, last - first)]
-            sends.append(
-                pltpu.make_async_remote_copy(
-                    part, part, tops_send.at[message, i], tops_recv.at[message, i],
-                    device_id={"zero": other}, device_id_type=MESH,
-                )
-            )
-            sends[-1].start()
-        return sends
-
-    def divide(e):
-        top = jnp.max(tops[:, e], axis=0)
+        return lax.fori_loop(0, groups, body, jnp.zeros((8, lanes), F32), unroll=8)
+
+    def remote(part, send_semaphore, recv_semaphore, other):
+        return pltpu.make_async_remote_copy(
+            part, part, send_semaphore, recv_semaphore, device_id=other, device_id_type=MESH
+        )
+
+    def to_all(values, message):
+        for other in others:
+            remote(values.at[me], tops_send.at[message], tops_recv.at[message], {"zero": other}).start()
+
+        return remote(
+            values.at[pl.ds(0, PLANE - 1)], tops_send.at[message], tops_recv.at[message], {"zero": me}
+        )
+
+    def divide(e, top):
         columns[e] = top
         inverse[...] = 1.0 / top
 
@@ -158,92 +172,58 @@
 
         lax.fori_loop(0, groups // 4, body, 0, unroll=2)
 
-    find_tops(0)
-    pl.semaphore_wait(barrier, PLANE - 1 + 3)
-    top_sends = share_tops(0, 1, 0)
-    for e in range(1, experts):
-        find_tops(e)
+    shared = []
+    for e in range(experts):
+        tops[e, me] = find_tops(e)
+        if e == 0:
+            pl.semaphore_wait(barrier, PLANE - 1 + flag(floor > 0) + flag(floor == last) + core)
+        shared.append(to_all(tops.at[e], e))
     for load in small:
         load.wait()
-    tops[me, experts, 0:4, :] = weight_in[...] * gain_in[...]
-    tops[me, experts, 4:8, :] = jnp.zeros((4, lanes), F32)
-    late_sends = share_tops(1, experts + 1, 1)
-
-    in_flight = []
+    part_router[me] = weight_in[...] * gain_in[...]
+    shared.append(to_all(part_router, experts))
 
     def send(direction, turn):
         piece, (x, y) = ORDER[direction][turn]
         part = slab.at[at(x, y), pl.ds(piece * per_piece, per_piece)]
-        copy = pltpu.make_async_remote_copy(
-            part, part, send_sem.at[direction, turn], recv_sem.at[direction, turn],
-            device_id={"zero": neighbour[direction]}, device_id_type=MESH,
-        )
-        copy.start()
-        in_flight.append(copy)
-
-    def receive(direction, turn):
-        piece, origin = ORDER[direction][turn]
-        x, y = (o + s for o, s in zip(origin, STEP[direction]))
-        part = slab.at[at(x + SIDE, y + SIDE), pl.ds(piece * per_piece, per_piece)]
-        pltpu.make_async_remote_copy(
-            part, part, send_sem.at[direction, turn], recv_sem.at[direction, turn],
-            device_id={"zero": neighbour[direction]}, device_id_type=MESH,
-        ).wait_recv()
-
-    done = 0
-
-    def ready(upto):
-        nonlocal done
-        while done < min(upto, experts):
-            if done < 2:
-                for copy in (top_sends, late_sends)[done]:
-                    copy.wait_recv()
-            divide(done)
-            done += 1
-
-    for turn in range(LEAD):
-        needed = max(ORDER[d][turn][0] for d in range(4) if ORDER[d][turn][1] == (0, 0))
-        ready(needed * per_piece // rows + 1)
-        for direction in range(4):
-            send(direction, turn)
-    ready(experts)
-
-    ring_copies, pair_copies = [], []
+        remote(part, send_sem, recv_sem.at[turn], {"zero": neighbour[direction]}).start()
+
+    def receive(turn):
+        part = slab.at[0, pl.ds(0, 4 * per_piece)]
+        remote(part, send_sem, recv_sem.at[turn], {"zero": me}).wait_recv()
+
+    for e in range(experts):
+        shared[e].wait_recv()
+        divide(e, jnp.max(tops[e], axis=0))
+        for turn in range(2 * e, min(2 * e + 2, LEAD)):
+            for direction in range(4):
+                send(direction, turn)
 
     def own_bank():
         for j in range(PLANE):
-            banks[bank, :, lanes * j : lanes * (j + 1)] = tops[j, experts, 0:4, :]
+            banks[bank, :, lanes * j : lanes * (j + 1)] = part_router[j]
 
     def bank_at(shift):
         return lax.rem(bank + bank_count + shift, bank_count)
 
+    ring_copies = []
+    pairs = remote(banks.at[pl.ds(0, bank_count // 2)], pair_send, pair_recv, {"bank": bank})
+
     def ring(step):
         for way, shift, other in ((0, -2, above), (1, 2, below)):
-            if step > (4 if way == 0 else 3):
-                continue
-            part = banks.at[bank_at(shift * (step - 1))]
-            copy = pltpu.make_async_remote_copy(
-                part, part, ring_send.at[way, step - 1], ring_recv.at[way, step - 1],
-                device_id={"bank": other}, device_id_type=MESH,
-            )
-            copy.start()
-            ring_copies.append(copy)
+            if step <= bank_count // 4 - way:
+                part = banks.at[bank_at(shift * (step - 1))]
+                copy = remote(part, ring_send, ring_recv.at[way, step - 1], {"bank": other})
+                copy.start()
+                ring_copies.append((step, copy))
 
     def ring_arrived(step):
-        for copy in ring_copies[2 * (step - 1) : 2 * step]:
-            copy.wait_recv()
-
-    def pair(step):
-        shifts = (0,) if step == 0 else (-2 * step, 2 * step) if step < 4 else (-2 * step,)
-        for shift in shifts:
-            part = banks.at[bank_at(shift)]
-            n = len(pair_copies)
-            copy = pltpu.make_async_remote_copy(
-                part, part, pair_send.at[n], pair_recv.at[n],
-                device_id={"bank": partner}, device_id_type=MESH,
-            )
-            copy.start()
-            pair_copies.append(copy)
+        for when, copy in ring_copies:
+            if when == step:
+                copy.wait_recv()
+
+    def pair(shift):
+        remote(banks.at[bank_at(shift)], pair_send, pair_recv, {"bank": partner}).start()
 
     def finish_scale():
         for e in range(experts):
@@ -257,27 +237,40 @@
                 scale_out[e : e + 1, lanes * r : lanes * (r + 1)] = line[r : r + 1, :]
 
     def finish_router():
-        for copy in pair_copies:
-            copy.wait_recv()
+        pairs.wait_recv()
         for b in range(bank_count):
             router_out[4 * b : 4 * b + 4, :] = banks[b]
 
     def ring_step(step):
         def run():
             ring_arrived(step)
+            ring(step + 1)
+            pair(-2 * step)
             if step < 4:
-                ring(step + 1)
-            pair(step)
+                pair(2 * step)
 
         return run
 
+    def say_hello():
+        greet(hello, floor > 0, below)
+        greet(hello, floor == last, above)
+        greet(hello, core == 1, partner)
+
     def first_step():
+        shared[experts].wait_recv()
         own_bank()
+        greeted = flag(floor < last) + flag(floor == 0) + 1 - core
+
+        @pl.when(greeted > 0)
+        def _():
+            pl.semaphore_wait(hello, greeted)
+
         ring(1)
         pair(0)
 
     every = TURNS // 10
     extras = {
+        0: say_hello,
         1: finish_scale,
         every: first_step,
         2 * every: ring_step(1),
@@ -288,39 +281,41 @@
     }
 
     for turn in range(TURNS):
-        for direction in range(4):
-            receive(direction, turn)
+        receive(turn)
         if turn + LEAD < TURNS:
             for direction in range(4):
                 send(direction, turn + LEAD)
         if turn in extras:
             extras[turn]()
-    for copy in in_flight + top_sends + late_sends + ring_copies + pair_copies:
+    remote(slab.at[pl.ds(0, PLANE - 1)], send_sem, recv_sem.at[0], {"zero": me}).wait_send()
+    for copy in shared:
         copy.wait_send()
+    remote(
+        banks.at[pl.ds(0, bank_count // 2 - 1)], ring_send, ring_recv.at[0, 0], {"bank": bank}
+    ).wait_send()
+    pairs.wait_send()
 
 
 def store(slab, scale_in, router_in, final, scale, router, half, sem):
     experts, rows, width = final.shape
     lanes = width // PLANE
-    copies = []
     for e in range(experts):
         for j in range(PLANE):
-            copies.append(
-                pltpu.make_async_copy(
-                    slab.at[j, pl.ds(e * rows, rows)],
-                    final.at[e, :, pl.ds(j * lanes, lanes)],
-                    sem.at[e * PLANE + j],
-                )
-            )
-    for copy in copies:
+            pltpu.make_async_copy(
+                slab.at[j, pl.ds(e * rows, rows)],
+                final.at[e, :, pl.ds(j * lanes, lanes)],
+                sem.at[0],
+            ).start()
+    half[...] = router_in[...].astype(BF16)
+    small = (
+        pltpu.make_async_copy(scale_in, scale, sem.at[1]),
+        pltpu.make_async_copy(half, router, sem.at[2]),
+    )
+    for copy in small:
         copy.start()
-    half[...] = router_in[...].astype(BF16)
-    copies.append(pltpu.make_async_copy(scale_in, scale, sem.at[experts * PLANE]))
-    copies.append(pltpu.make_async_copy(half, router, sem.at[experts * PLANE + 1]))
-    copies[-2].start()
-    copies[-1].start()
-    for copy in copies:
+    for copy in small:
         copy.wait()
+    pltpu.make_async_copy(slab, slab, sem.at[0]).wait()
 
 
 def shards(master, second, weight, gain):
@@ -345,20 +340,22 @@
             pltpu.VMEM((experts, rows, lanes), BF16),
             pltpu.VMEM((experts, lanes), F32),
             pltpu.VMEM((1, lanes), F32),
-            pltpu.VMEM((PLANE, experts + 1, 8, lanes), F32),
+            pltpu.VMEM((experts, PLANE, 8, lanes), F32),
+            pltpu.VMEM((PLANE, experts, lanes), F32),
             pltpu.VMEM((8, lanes), F32),
             pltpu.VMEM((experts, 8, lanes), F32),
             pltpu.VMEM((banks, experts, width), F32),
             pltpu.VMEM((lanes, lanes), F32),
             dma((2 * experts + 2,)),
-            dma((2, PLANE - 1)),
-            dma((2, PLANE - 1)),
-            dma((4, TURNS)),
-            dma((4, TURNS)),
-            dma((2, 4)),
-            dma((2, 4)),
-            dma((8,)),
-            dma((8,)),
+            dma((experts + 1,)),
+            dma((experts + 1,)),
+            pltpu.SemaphoreType.REGULAR,
+            dma,
+            dma((TURNS,)),
+            dma,
+            dma((2, banks // 4)),
+            dma,
+            dma,
         ],
         compiler_params=pltpu.CompilerParams(
             collective_id=0, has_side_effects=True, vmem_limit_bytes=24 << 20
@@ -376,7 +373,7 @@
         out_specs=(hbm,) * 3,
         scratch_shapes=[
             pltpu.VMEM((banks * experts, width), BF16),
-            dma((experts * PLANE + 2,)),
+            dma((3,)),
         ],
         compiler_params=pltpu.CompilerParams(vmem_limit_bytes=4 << 20),
         name="store",

time: 111 us -> 104 us (0.937)
  Pallas kernels: 110 us -> 103 us
    pallas_call x1, Pallas kernels: 103 us -> 97 us  [shards(): pl.pallas_call(exchange, out_shape=(pltpu.VMEM((PLANE, experts * rows, la...]
where the time goes in v2:
time: 104 us; the launch traced here: 103 us
  Pallas kernels  103 us (99%)
    pallas_call x1, Pallas kernels, shards(): pl.pallas_call(exchange, out_shape=(pltpu.VMEM((PLANE, experts * rows, la...  97 us
    pallas_call x1, Pallas kernels, shards(): pl.pallas_call(store, out_shape=(jax.ShapeDtypeStruct((experts, rows, wid...  5.88 us

profile of v2, /device:TPU:2, one launch (start us, length us, event | category | flops | bytes accessed | tf_op | source)
XLA Modules:
  0.0 103.5 jit_solution(6371441768517863433)
XLA Ops:
  0.6 97.0 %exchange.1 = (bf16[16,4096,128]{2,1,0:T(8,128)(2,1)S(1)}, f32[4,1024]{1,0:T(4,128)S(1)}, f32[64,2048]{1,0:T(8,128)S(1)}) custom-call(f32[4,1024,128]{2,1,0:T(8,128)} %master.1, bf16[4,1024,128]{2,1,0:T(8,128)(2,1)} %second.1, f32[4,128]{1,0:T(4,128)} %bitcast.3, f32[1,128]{1,0:T(1,128)} %bitcast.4), custom_call_target="tpu_custom_call" | custom-call | tf_op jit(solution)/shard_map/exchange/pallas_call | solution.py:329
  97.6 5.9 %store.1 = (bf16[4,1024,2048]{2,1,0:T(8,128)(2,1)}, f32[4,1024]{1,0:T(4,128)}, bf16[64,2048]{1,0:T(8,128)(2,1)}) custom-call(bf16[16,4096,128]{2,1,0:T(8,128)(2,1)S(1)} %get-tuple-element.9.slab, f32[4,1024]{1,0:T(4,128)S(1)} %get-tuple-element.10.scale_in, f32[64,2048]{1,0:T(8,128)S(1)} %get-tuple-element.11.router_in), custom_call_target="tpu_custom_call" | custom-call | tf_op jit(solution)/shard_map/store/pallas_call | solution.py:365

commit v3 on v2

--- a/solution.py
+++ b/solution.py
@@ -107,7 +107,9 @@
         load.start()
 
     barrier = pltpu.get_barrier_semaphore()
-    others = [at(x, y) for y in range(SIDE) for x in range(SIDE) if (x, y) != (0, 0)]
+    hops = [min(step, SIDE - step) for step in range(SIDE)]
+    offsets = [(x, y) for y in range(SIDE) for x in range(SIDE) if (x, y) != (0, 0)]
+    others = [at(x, y) for x, y in sorted(offsets, key=lambda o: -hops[o[0]] - hops[o[1]])]
     for other in others:
         pl.semaphore_signal(barrier, inc=1, device_id={"zero": other}, device_id_type=MESH)
     floor, core = lax.div(bank, 2), lax.rem(bank, 2)
@@ -140,7 +142,7 @@
             top = jnp.where(lane == 2 * g, peak[:8], top)
             return jnp.where(lane == 2 * g + 1, peak[8:], top)
 
-        return lax.fori_loop(0, groups, body, jnp.zeros((8, lanes), F32), unroll=8)
+        return lax.fori_loop(0, groups, body, jnp.zeros((8, lanes), F32), unroll=32)
 
     def remote(part, send_semaphore, recv_semaphore, other):
         return pltpu.make_async_remote_copy(
@@ -170,7 +172,7 @@
                 slab[me, to_rows, :] = value.astype(BF16)
             return carry
 
-        lax.fori_loop(0, groups // 4, body, 0, unroll=2)
+        lax.fori_loop(0, groups // 4, body, 0, unroll=8)
 
     shared = []
     for e in range(experts):

time: 104 us -> 103 us (level)
  no operation moved by 1% of the time
where the time goes in v3:
time: 103 us
  Pallas kernels  102 us (99%)
    pallas_call x1, Pallas kernels, shards(): pl.pallas_call(exchange, out_shape=(pltpu.VMEM((PLANE, experts * rows, la...  96.1 us
    pallas_call x1, Pallas kernels, shards(): pl.pallas_call(store, out_shape=(jax.ShapeDtypeStruct((experts, rows, wid...  5.88 us

profile of v3, /device:TPU:2, one launch (start us, length us, event | category | flops | bytes accessed | tf_op | source)
XLA Modules:
  0.0 102.6 jit_solution(14472672279017671866)
XLA Ops:
  0.6 96.1 %exchange.1 = (bf16[16,4096,128]{2,1,0:T(8,128)(2,1)S(1)}, f32[4,1024]{1,0:T(4,128)S(1)}, f32[64,2048]{1,0:T(8,128)S(1)}) custom-call(f32[4,1024,128]{2,1,0:T(8,128)} %master.1, bf16[4,1024,128]{2,1,0:T(8,128)(2,1)} %second.1, f32[4,128]{1,0:T(4,128)} %bitcast.3, f32[1,128]{1,0:T(1,128)} %bitcast.4), custom_call_target="tpu_custom_call" | custom-call | tf_op jit(solution)/shard_map/exchange/pallas_call | solution.py:331
  96.7 5.9 %store.1 = (bf16[4,1024,2048]{2,1,0:T(8,128)(2,1)}, f32[4,1024]{1,0:T(4,128)}, bf16[64,2048]{1,0:T(8,128)(2,1)}) custom-call(bf16[16,4096,128]{2,1,0:T(8,128)(2,1)S(1)} %get-tuple-element.9.slab, f32[4,1024]{1,0:T(4,128)S(1)} %get-tuple-element.10.scale_in, f32[64,2048]{1,0:T(8,128)S(1)} %get-tuple-element.11.router_in), custom_call_target="tpu_custom_call" | custom-call | tf_op jit(solution)/shard_map/store/pallas_call | solution.py:367

commit v4 on v3

--- a/solution.py
+++ b/solution.py
@@ -8,8 +8,9 @@
 SIDE = 4
 PLANE = SIDE * SIDE
 EXPERTS = 4
-PIECES = 8
-LEAD = 4
+PIECES = 16
+LATE = 5
+LEAD = 10
 MESH = pl.DeviceIdType.MESH
 F32 = jnp.float32
 BF16 = jnp.bfloat16
@@ -39,40 +40,50 @@
 def schedule():
     waiting = [[] for _ in range(4)]
     order = [[] for _ in range(4)]
+    events = []
     for piece in range(PIECES):
         for direction, weight in routes(piece, (0, 0), None):
             waiting[direction].append((-weight, 0, piece, (0, 0)))
 
-    def pick():
-        for direction in range(4):
-            limit = (len(order[direction]) // 2 + 1) * PIECES // EXPERTS
-            now = [entry for entry in waiting[direction] if entry[2] < limit or entry[1]]
-            if now:
-                best = min(now)
-                waiting[direction].remove(best)
-                order[direction].append(best[2:])
-
-    for _ in range(LEAD):
-        pick()
+    def pick(turn):
+        limit = (max(0, turn - LATE + 1) + 1) * PIECES // EXPERTS
+        now = []
+        for depth in range(turn + 1, turn + 1 + LEAD):
+            for direction in range(4):
+                if len(order[direction]) > depth:
+                    continue
+                ready = [entry for entry in waiting[direction] if entry[2] < limit or entry[1]]
+                if turn < 0:
+                    ready = [entry for entry in ready if entry[2] <= depth]
+                if ready:
+                    best = min(ready)
+                    waiting[direction].remove(best)
+                    now.append((direction, len(order[direction])))
+                    order[direction].append(best[2:])
+        events.append(now)
+
+    pick(-1)
     for turn in range((PLANE - 1) * PIECES // 4):
         for direction in range(4):
             piece, origin = order[direction][turn]
             origin = tuple((o + s) % SIDE for o, s in zip(origin, STEP[direction]))
             for onward, weight in routes(piece, origin, direction):
                 waiting[onward].append((-weight, turn + 1, piece, origin))
-        pick()
-    return order
-
-
-ORDER = schedule()
+        pick(turn)
+    return order, events
+
+
+ORDER, EVENTS = schedule()
 TURNS = (PLANE - 1) * PIECES // 4
 assert all(len(lane) == TURNS for lane in ORDER)
+assert all(lane[0] == (0, (0, 0)) for lane in ORDER)
 
 
 def exchange(
     master, second, weight, gain, slab, scale_out, router_out,
-    merged, change, weight_in, gain_in, tops, part_router, inverse, columns, banks, wide,
-    load_sem, tops_send, tops_recv, hello, send_sem, recv_sem, ring_send, ring_recv, pair_send, pair_recv,
+    merged, change, weight_in, gain_in, tops, tops_x, tops_y, early, part_router, inverse,
+    columns, banks, wide, load_sem, tops_send, tops_recv, axis_send, axis_recv, early_send,
+    hello, send_sem, recv_sem, ring_send, ring_recv, pair_send, pair_recv,
 ):
     experts, rows, lanes = master.shape
     per_piece = experts * rows // PIECES
@@ -157,33 +168,48 @@
             values.at[pl.ds(0, PLANE - 1)], tops_send.at[message], tops_recv.at[message], {"zero": me}
         )
 
+    def along(axis, values, mine):
+        for step in range(1, SIDE):
+            other = at(step, 0) if axis == 0 else at(0, step)
+            remote(values.at[mine], axis_send.at[axis], axis_recv.at[axis], {"zero": other}).start()
+        return remote(
+            values.at[pl.ds(0, SIDE - 1)], axis_send.at[axis], axis_recv.at[axis], {"zero": me}
+        )
+
+    def scaled(read, write, count):
+        def body(g, carry):
+            here = pltpu.roll(inverse[...], lax.rem(lanes - 8 * g, lanes), 1)
+            for i in range(4):
+                first = pl.multiple_of(g * 64 + 16 * i, 16)
+                low = jnp.broadcast_to(here[:, 2 * i : 2 * i + 1], (8, lanes))
+                high = jnp.broadcast_to(here[:, 2 * i + 1 : 2 * i + 2], (8, lanes))
+                value = read(first) * jnp.concatenate([low, high], axis=0)
+                write(first, value.astype(BF16))
+            return carry
+
+        lax.fori_loop(0, count // 64, body, 0, unroll=min(8, count // 64))
+
     def divide(e, top):
         columns[e] = top
         inverse[...] = 1.0 / top
 
-        def body(g, carry):
-            here = pltpu.roll(inverse[...], lax.rem(lanes - 8 * g, lanes), 1)
-            for i in range(4):
-                at_rows = pl.ds(pl.multiple_of(g * 64 + 16 * i, 16), 16)
-                low = jnp.broadcast_to(here[:, 2 * i : 2 * i + 1], (8, lanes))
-                high = jnp.broadcast_to(here[:, 2 * i + 1 : 2 * i + 2], (8, lanes))
-                value = merged[e, at_rows, :] * jnp.concatenate([low, high], axis=0)
-                to_rows = pl.ds(pl.multiple_of(e * rows + g * 64 + 16 * i, 16), 16)
-                slab[me, to_rows, :] = value.astype(BF16)
-            return carry
-
-        lax.fori_loop(0, groups // 4, body, 0, unroll=8)
-
-    shared = []
-    for e in range(experts):
-        tops[e, me] = find_tops(e)
-        if e == 0:
-            pl.semaphore_wait(barrier, PLANE - 1 + flag(floor > 0) + flag(floor == last) + core)
-        shared.append(to_all(tops.at[e], e))
-    for load in small:
-        load.wait()
-    part_router[me] = weight_in[...] * gain_in[...]
-    shared.append(to_all(part_router, experts))
+        def write(first, value):
+            slab[me, pl.ds(pl.multiple_of(e * rows + first, 16), 16), :] = value
+
+        scaled(lambda first: merged[e, pl.ds(first, 16), :], write, rows)
+
+    def came_from(direction, origin):
+        x, y = (o + s for o, s in zip(origin, STEP[direction]))
+        return at(x + SIDE, y + SIDE)
+
+    def divide_early():
+        for direction in range(4):
+            source = came_from(direction, (0, 0))
+
+            def write(first, value):
+                slab[source, pl.ds(first, 16), :] = value
+
+            scaled(lambda first: early[direction, pl.ds(first, 16), :], write, per_piece)
 
     def send(direction, turn):
         piece, (x, y) = ORDER[direction][turn]
@@ -194,12 +220,37 @@
         part = slab.at[0, pl.ds(0, 4 * per_piece)]
         remote(part, send_sem, recv_sem.at[turn], {"zero": me}).wait_recv()
 
-    for e in range(experts):
-        shared[e].wait_recv()
-        divide(e, jnp.max(tops[e], axis=0))
-        for turn in range(2 * e, min(2 * e + 2, LEAD)):
-            for direction in range(4):
+    tops[me] = find_tops(0)
+    pl.semaphore_wait(barrier, PLANE - 1 + flag(floor > 0) + flag(floor == last) + core)
+    shared = [to_all(tops, 0)]
+    for direction in range(4):
+        pltpu.make_async_remote_copy(
+            merged.at[0, pl.ds(0, per_piece)], early.at[direction], early_send, recv_sem.at[0],
+            device_id={"zero": neighbour[direction]}, device_id_type=MESH,
+        ).start()
+    for e in range(1, experts):
+        tops_x[my_x, e - 1] = find_tops(e)
+    by_axis = [along(0, tops_x, my_x)]
+    for load in small:
+        load.wait()
+    part_router[me] = weight_in[...] * gain_in[...]
+    shared.append(to_all(part_router, 1))
+
+    def send_all(events):
+        for direction, turn in events:
+            if turn:
                 send(direction, turn)
+
+    shared[0].wait_recv()
+    divide(0, jnp.max(tops[...], axis=0))
+    send_all(EVENTS[0])
+    all_early = remote(early, early_send, recv_sem.at[0], {"zero": me})
+    all_early.wait_recv()
+    divide_early()
+    send_all(EVENTS[1])
+    by_axis[0].wait_recv()
+    tops_y[my_y] = jnp.max(tops_x[...], axis=0)
+    by_axis.append(along(1, tops_y, my_y))
 
     def own_bank():
         for j in range(PLANE):
@@ -259,7 +310,7 @@
         greet(hello, core == 1, partner)
 
     def first_step():
-        shared[experts].wait_recv()
+        shared[1].wait_recv()
         own_bank()
         greeted = flag(floor < last) + flag(floor == 0) + 1 - core
 
@@ -270,27 +321,33 @@
         ring(1)
         pair(0)
 
+    def late(e):
+        if e == 1:
+            by_axis[1].wait_recv()
+        divide(e, jnp.max(tops_y[:, e - 1], axis=0))
+
     every = TURNS // 10
     extras = {
-        0: say_hello,
-        1: finish_scale,
-        every: first_step,
-        2 * every: ring_step(1),
-        3 * every: ring_step(2),
-        4 * every: ring_step(3),
-        5 * every: ring_step(4),
-        6 * every: finish_router,
+        1: say_hello,
+        LATE + 5: finish_scale,
+        LATE + 8: first_step,
+        4 * every: ring_step(1),
+        5 * every: ring_step(2),
+        6 * every: ring_step(3),
+        7 * every: ring_step(4),
+        8 * every: finish_router,
     }
 
-    for turn in range(TURNS):
+    for turn in range(1, TURNS):
         receive(turn)
-        if turn + LEAD < TURNS:
-            for direction in range(4):
-                send(direction, turn + LEAD)
+        if LATE <= turn < LATE + experts - 1:
+            late(turn - LATE + 1)
+        send_all(EVENTS[turn + 1])
         if turn in extras:
             extras[turn]()
-    remote(slab.at[pl.ds(0, PLANE - 1)], send_sem, recv_sem.at[0], {"zero": me}).wait_send()
-    for copy in shared:
+    turns = slab.reshape(PLANE * SIDE, experts * rows // SIDE, lanes)
+    remote(turns.at[pl.ds(0, TURNS - 1)], send_sem, recv_sem.at[0], {"zero": me}).wait_send()
+    for copy in [all_early, *shared, *by_axis]:
         copy.wait_send()
     remote(
         banks.at[pl.ds(0, bank_count // 2 - 1)], ring_send, ring_recv.at[0, 0], {"bank": bank}
@@ -342,15 +399,21 @@
             pltpu.VMEM((experts, rows, lanes), BF16),
             pltpu.VMEM((experts, lanes), F32),
             pltpu.VMEM((1, lanes), F32),
-            pltpu.VMEM((experts, PLANE, 8, lanes), F32),
+            pltpu.VMEM((PLANE, 8, lanes), F32),
+            pltpu.VMEM((SIDE, experts - 1, 8, lanes), F32),
+            pltpu.VMEM((SIDE, experts - 1, 8, lanes), F32),
+            pltpu.VMEM((4, experts * rows // PIECES, lanes), F32),
             pltpu.VMEM((PLANE, experts, lanes), F32),
             pltpu.VMEM((8, lanes), F32),
             pltpu.VMEM((experts, 8, lanes), F32),
             pltpu.VMEM((banks, experts, width), F32),
             pltpu.VMEM((lanes, lanes), F32),
             dma((2 * experts + 2,)),
-            dma((experts + 1,)),
-            dma((experts + 1,)),
+            dma((2,)),
+            dma((2,)),
+            dma((2,)),
+            dma((2,)),
+            dma,
             pltpu.SemaphoreType.REGULAR,
             dma,
             dma((TURNS,)),

time: 103 us -> 103 us (level)
  no operation moved by 1% of the time
where the time goes in v4:
time: 103 us; the launch traced here: 102 us
  Pallas kernels  101 us (98%)
    pallas_call x1, Pallas kernels, shards(): pl.pallas_call(exchange, out_shape=(pltpu.VMEM((PLANE, experts * rows, la...  95.5 us
    pallas_call x1, Pallas kernels, shards(): pl.pallas_call(store, out_shape=(jax.ShapeDtypeStruct((experts, rows, wid...  5.88 us

profile of v4, /device:TPU:2, one launch (start us, length us, event | category | flops | bytes accessed | tf_op | source)
XLA Modules:
  0.0 102.1 jit_solution(16404874964174115200)
XLA Ops:
  0.6 95.5 %exchange.1 = (bf16[16,4096,128]{2,1,0:T(8,128)(2,1)S(1)}, f32[4,1024]{1,0:T(4,128)S(1)}, f32[64,2048]{1,0:T(8,128)S(1)}) custom-call(f32[4,1024,128]{2,1,0:T(8,128)} %master.1, bf16[4,1024,128]{2,1,0:T(8,128)(2,1)} %second.1, f32[4,128]{1,0:T(4,128)} %bitcast.3, f32[1,128]{1,0:T(1,128)} %bitcast.4), custom_call_target="tpu_custom_call" | custom-call | tf_op jit(solution)/shard_map/exchange/pallas_call | solution.py:388
  96.2 5.9 %store.1 = (bf16[4,1024,2048]{2,1,0:T(8,128)(2,1)}, f32[4,1024]{1,0:T(4,128)}, bf16[64,2048]{1,0:T(8,128)(2,1)}) custom-call(bf16[16,4096,128]{2,1,0:T(8,128)(2,1)S(1)} %get-tuple-element.9.slab, f32[4,1024]{1,0:T(4,128)S(1)} %get-tuple-element.10.scale_in, f32[64,2048]{1,0:T(8,128)S(1)} %get-tuple-element.11.router_in), custom_call_target="tpu_custom_call" | custom-call | tf_op jit(solution)/shard_map/store/pallas_call | solution.py:430

commit v5 on v4

--- a/solution.py
+++ b/solution.py
@@ -10,6 +10,7 @@
 EXPERTS = 4
 PIECES = 16
 LATE = 5
+ALONE, SPAN = 8, 2
 LEAD = 10
 MESH = pl.DeviceIdType.MESH
 F32 = jnp.float32
@@ -37,6 +38,12 @@
 STEP = ((-1, 0), (1, 0), (0, -1), (0, 1))
 
 
+TURNS = (PLANE - 1) * PIECES // 4
+GROUPS = [[turn] for turn in range(ALONE)]
+GROUPS += [list(range(turn, turn + SPAN)) for turn in range(ALONE, TURNS, SPAN)]
+PLACE = {turn: place for place, group in enumerate(GROUPS) for turn in group}
+
+
 def schedule():
     waiting = [[] for _ in range(4)]
     order = [[] for _ in range(4)]
@@ -63,18 +70,18 @@
         events.append(now)
 
     pick(-1)
-    for turn in range((PLANE - 1) * PIECES // 4):
-        for direction in range(4):
-            piece, origin = order[direction][turn]
-            origin = tuple((o + s) % SIDE for o, s in zip(origin, STEP[direction]))
-            for onward, weight in routes(piece, origin, direction):
-                waiting[onward].append((-weight, turn + 1, piece, origin))
-        pick(turn)
+    for group in GROUPS:
+        for turn in group:
+            for direction in range(4):
+                piece, origin = order[direction][turn]
+                origin = tuple((o + s) % SIDE for o, s in zip(origin, STEP[direction]))
+                for onward, weight in routes(piece, origin, direction):
+                    waiting[onward].append((-weight, turn + 1, piece, origin))
+        pick(group[-1])
     return order, events
 
 
 ORDER, EVENTS = schedule()
-TURNS = (PLANE - 1) * PIECES // 4
 assert all(len(lane) == TURNS for lane in ORDER)
 assert all(lane[0] == (0, (0, 0)) for lane in ORDER)
 
@@ -214,11 +221,12 @@
     def send(direction, turn):
         piece, (x, y) = ORDER[direction][turn]
         part = slab.at[at(x, y), pl.ds(piece * per_piece, per_piece)]
-        remote(part, send_sem, recv_sem.at[turn], {"zero": neighbour[direction]}).start()
-
-    def receive(turn):
-        part = slab.at[0, pl.ds(0, 4 * per_piece)]
-        remote(part, send_sem, recv_sem.at[turn], {"zero": me}).wait_recv()
+        semaphore = recv_sem.at[PLACE[turn]]
+        remote(part, send_sem, semaphore, {"zero": neighbour[direction]}).start()
+
+    def receive(place):
+        part = slab.at[0, pl.ds(0, 4 * per_piece * len(GROUPS[place]))]
+        remote(part, send_sem, recv_sem.at[place], {"zero": me}).wait_recv()
 
     tops[me] = find_tops(0)
     pl.semaphore_wait(barrier, PLANE - 1 + flag(floor > 0) + flag(floor == last) + core)
@@ -338,13 +346,15 @@
         8 * every: finish_router,
     }
 
-    for turn in range(1, TURNS):
-        receive(turn)
-        if LATE <= turn < LATE + experts - 1:
-            late(turn - LATE + 1)
-        send_all(EVENTS[turn + 1])
-        if turn in extras:
-            extras[turn]()
+    for place, group in list(enumerate(GROUPS))[1:]:
+        receive(place)
+        for turn in group:
+            if LATE <= turn < LATE + experts - 1:
+                late(turn - LATE + 1)
+        send_all(EVENTS[place + 1])
+        for turn in group:
+            if turn in extras:
+                extras[turn]()
     turns = slab.reshape(PLANE * SIDE, experts * rows // SIDE, lanes)
     remote(turns.at[pl.ds(0, TURNS - 1)], send_sem, recv_sem.at[0], {"zero": me}).wait_send()
     for copy in [all_early, *shared, *by_axis]:
@@ -416,7 +426,7 @@
             dma,
             pltpu.SemaphoreType.REGULAR,
             dma,
-            dma((TURNS,)),
+            dma((len(GROUPS),)),
             dma,
             dma((2, banks // 4)),
             dma,

time: 103 us -> 102 us (level)
  no operation moved by 1% of the time
where the time goes in v5:
time: 102 us
  Pallas kernels  101 us (99%)
    pallas_call x1, Pallas kernels, shards(): pl.pallas_call(exchange, out_shape=(pltpu.VMEM((PLANE, experts * rows, la...  95.3 us
    pallas_call x1, Pallas kernels, shards(): pl.pallas_call(store, out_shape=(jax.ShapeDtypeStruct((experts, rows, wid...  5.88 us

profile of v5, /device:TPU:2, one launch (start us, length us, event | category | flops | bytes accessed | tf_op | source)
XLA Modules:
  0.0 101.8 jit_solution(2165892103913607055)
XLA Ops:
  0.6 95.3 %exchange.1 = (bf16[16,4096,128]{2,1,0:T(8,128)(2,1)S(1)}, f32[4,1024]{1,0:T(4,128)S(1)}, f32[64,2048]{1,0:T(8,128)S(1)}) custom-call(f32[4,1024,128]{2,1,0:T(8,128)} %master.1, bf16[4,1024,128]{2,1,0:T(8,128)(2,1)} %second.1, f32[4,128]{1,0:T(4,128)} %bitcast.3, f32[1,128]{1,0:T(1,128)} %bitcast.4), custom_call_target="tpu_custom_call" | custom-call | tf_op jit(solution)/shard_map/exchange/pallas_call | solution.py:398
  96.0 5.9 %store.1 = (bf16[4,1024,2048]{2,1,0:T(8,128)(2,1)}, f32[4,1024]{1,0:T(4,128)}, bf16[64,2048]{1,0:T(8,128)(2,1)}) custom-call(bf16[16,4096,128]{2,1,0:T(8,128)(2,1)S(1)} %get-tuple-element.9.slab, f32[4,1024]{1,0:T(4,128)S(1)} %get-tuple-element.10.scale_in, f32[64,2048]{1,0:T(8,128)S(1)} %get-tuple-element.11.router_in), custom_call_target="tpu_custom_call" | custom-call | tf_op jit(solution)/shard_map/store/pallas_call | solution.py:440
